TPU v7x, 256 devices: a whole 4x4x8 slice. The times are simulated.
256 devices in a mesh: enc: 32 (over z, x), tp: 8 (over y, core).
Axes of the slice: x: 4, y: 4, z: 8, core: 2. Of those that a mesh axis runs over, the one named last changes fastest.
Arguments:
- grad_rows: bfloat16 [20480, 8192], P('enc', 'tp'), may hold values from -6 to 6
- features: bfloat16 [20480, 1280], P('enc'), may hold values from -6 to 6
- block_in: bfloat16 [20480, 1280], P('enc', 'tp'), may hold values from -6 to 6
- patch_counts: int32 [32, 5], replicated, may hold values from 32 to 128, as said below
- owner: int32 [32, 5], replicated, may hold values from 0 to 31, as said below
- ln1_gain: float32 [1280], replicated, may hold values from 0.5 to 1.5
- w_qkv: bfloat16 [1280, 16, 240], P(None, 'tp')
- w_out: bfloat16 [1280, 1280], P('tp'), may hold values from -0.15625 to 0.15625
- w_proj: bfloat16 [1280, 8192], P(None, 'tp'), may hold values from -0.15625 to 0.15625
Outputs:
- grad_input: bfloat16 [20480, 1280], P('enc', 'tp')
- grad_proj: float32 [1280, 8192], P('enc', 'tp')
- grad_qkv: float32 [1280, 16, 240], P('enc', 'tp')
- grad_out: float32 [1280, 1280], P('tp', 'enc')
- grad_ln1: float32 [1280], P('enc')
Inputs may be any that keep to these rules, and one draw needn't show every extreme that they name: `patch_counts`: some image has exactly 128 live rows and some exactly 32. `owner`: each encoder device receives exactly 5 images, never two from the same block.
All inputs are finite; a program needn't handle non-finite values.
Results may differ from a plain program's by a relative error of at most 0.033.
Values may be sent and summed in bfloat16 or wider, within the bound.
No kernel may reach another device: no remote copies, remote signals or barrier semaphores. Data moves between devices by JAX's collectives and lax.ppermute only.
A program may use at most 64 MiB of HBM per device.

v0:
```python
import jax
import jax.numpy as jnp
from jax import lax
from jax.sharding import Mesh
from jax.sharding import PartitionSpec as P

TILE = 128
ENC = ("enc_0", "enc_1")


EPSILON = 1e-05


def from_everyone(shard, axis):
    copies = jnp.broadcast_to(shard, (lax.axis_size(axis), *shard.shape))
    return lax.all_to_all(copies, axis, split_axis=0, concat_axis=0, tiled=True)


def in_order(blocks, dim):
    shape = list(blocks.shape[1:])
    shape[dim] *= blocks.shape[0]
    return jnp.moveaxis(blocks, 0, dim).reshape(shape)


def gathered_copies(shard, axis, dim):
    blocks = from_everyone(shard, axis)
    return in_order(blocks, dim)


def in_blocks(shard, dim, devices):
    before, after = (shard.shape[:dim], shard.shape[dim + 1 :])
    return jnp.moveaxis(shard.reshape(*before, devices, -1, *after), dim, 0)


def summed_on_arrival(shard, axis, dim):
    blocks = in_blocks(shard, dim, lax.axis_size(axis))
    arrived = lax.all_to_all(blocks, axis, split_axis=0, concat_axis=0, tiled=True)
    return arrived.astype(jnp.float32).sum(axis=0)


def summed_rows(shard, axes, dim):
    if not axes:
        return shard
    nearer = lax.psum_scatter(shard, axes[0], scatter_dimension=dim, tiled=True)
    return summed_rows(nearer, axes[1:], dim)


def of_everyone(shard, axis):
    return from_everyone(shard, axis).sum(axis=0)


def in_one(arrays, axis):
    ends = [0]
    for a in arrays:
        ends.append(ends[-1] + a.size)
    subtotal = of_everyone(jnp.concatenate([a.ravel() for a in arrays]), axis)
    return tuple((subtotal[b:e].reshape(a.shape) for a, b, e in zip(arrays, ends, ends[1:])))


def one_scatter(arrays, axis, dims):
    devices = lax.axis_size(axis)
    blocks = [in_blocks(a, dim, devices) for a, dim in zip(arrays, dims)]
    lines = jnp.concatenate([b.reshape(devices, -1) for b in blocks], axis=1)
    rows = max(16, -(-lines.shape[1] // 1024) * 8)
    lines = jnp.pad(lines, ((0, 0), (0, rows * 128 - lines.shape[1]))).reshape(-1, 128)
    line, at, gathered = (lax.psum_scatter(lines, axis, tiled=True).reshape(-1), 0, [])
    for b in blocks:
        part = b[0]
        gathered.append(line[at : at + part.size].reshape(part.shape))
        at += part.size
    return tuple(gathered)


def normalize(values):
    centred = values - jnp.mean(values, axis=-1, keepdims=True)
    variance = jnp.mean(centred * centred, axis=-1, keepdims=True)
    inverse = lax.rsqrt(variance + EPSILON)
    return (centred * inverse, inverse)


def dot_nt(left, right):
    return lax.dot_general(
        left, right, (((1,), (1,)), ((), ())), preferred_element_type=jnp.float32
    )


def dot_tn(left, right):
    return lax.dot_general(
        left, right, (((0,), (0,)), ((), ())), preferred_element_type=jnp.float32
    )


def shards(grad_rows, features, block_in, patch_counts, owner, ln1_gain, w_qkv, w_out, w_proj):
    groups = lax.axis_size(ENC)
    device = lax.axis_index(ENC)
    tp_rank = lax.axis_index("tp")
    block_rows = grad_rows.shape[0]
    img_group = block_rows // TILE
    block_full = gathered_copies(block_in, "tp", 1)
    line_index = jnp.arange(TILE, dtype=jnp.int32)
    peer_index = jnp.arange(groups, dtype=jnp.int32)
    own_counts = lax.dynamic_index_in_dim(patch_counts, device, 0, keepdims=False)
    own_owner = lax.dynamic_index_in_dim(owner, device, 0, keepdims=False)
    live_own = line_index[None, :] < own_counts[:, None]
    sends = jnp.any(owner == device, axis=1)
    sends_int = sends.astype(jnp.int32)
    rank = jnp.cumsum(sends_int) - sends_int
    slot_index = jnp.arange(img_group, dtype=jnp.int32)
    source_of = jnp.sum(
        jnp.where(sends[None, :] & (rank[None, :] == slot_index[:, None]), peer_index[None, :], 0),
        axis=1,
    )
    source_owner = jnp.take(owner, source_of, axis=0)
    source_counts = jnp.take(patch_counts, source_of, axis=0)
    arrived_counts = jnp.sum(jnp.where(source_owner == device, source_counts, 0), axis=1)
    live_tiles = line_index[None, :] < arrived_counts[:, None]
    shared = summed_on_arrival(dot_nt(grad_rows, w_proj).astype(jnp.bfloat16), "tp", 1)
    columns = shared.shape[1]
    tiles = shared.reshape(img_group, TILE, columns)
    tiles = jnp.where(live_own[:, :, None], tiles, jnp.zeros_like(tiles))
    received = lax.all_to_all(
        jnp.zeros((groups, TILE, columns), shared.dtype)
        .at[own_owner]
        .set(tiles)
        .astype(jnp.bfloat16),
        ENC,
        split_axis=0,
        concat_axis=0,
        tiled=True,
    ).astype(jnp.float32)
    vis_grad = lax.all_gather(
        jnp.take(received, source_of, axis=0)
        .reshape(block_rows, received.shape[2])
        .astype(jnp.bfloat16),
        "tp",
        axis=1,
        tiled=True,
    ).astype(jnp.float32)
    kept_rows = jnp.where(live_own.reshape(-1)[:, None], features, jnp.zeros_like(features))
    proj_term = dot_tn(kept_rows, grad_rows)
    grad_proj = summed_rows(proj_term.astype(jnp.bfloat16), ENC, 0).astype(jnp.float32)
    features_dim = block_full.shape[1]
    heads_here = w_qkv.shape[1]
    head_size = w_qkv.shape[2] // 3
    rows_here = block_full.shape[0]
    qkv_flat = w_qkv.reshape(features_dim, heads_here * 3 * head_size)
    normed1, inverse1 = normalize(block_full.astype(jnp.float32))
    normed_in = (normed1 * ln1_gain).astype(jnp.bfloat16)
    packed = jnp.dot(normed_in, qkv_flat, preferred_element_type=jnp.float32).astype(jnp.bfloat16)
    packed = packed.reshape(img_group, TILE, heads_here, 3, head_size)
    queries = packed[:, :, :, 0, :]
    keys_part = packed[:, :, :, 1, :]
    values_part = packed[:, :, :, 2, :]
    scaling = 1.0 / head_size**0.5
    scores = (
        jnp.einsum("gqhd,gkhd->ghqk", queries, keys_part, preferred_element_type=jnp.float32)
        * scaling
    )
    same_kind = (live_tiles[:, :, None] == live_tiles[:, None, :])[:, None]
    scores = jnp.where(same_kind, scores, -1e30)
    row_max = jnp.max(scores, axis=-1, keepdims=True)
    exp_terms = jnp.exp(scores - row_max)
    probability = exp_terms / jnp.sum(exp_terms, axis=-1, keepdims=True)
    prob_low = probability.astype(jnp.bfloat16)
    mixed = jnp.einsum(
        "ghqk,gkhd->gqhd", prob_low, values_part, preferred_element_type=jnp.float32
    ).astype(jnp.bfloat16)
    mixed = mixed.reshape(rows_here, heads_here * head_size)
    middle_b = vis_grad.astype(jnp.bfloat16)
    out_term = dot_tn(mixed, middle_b)
    mixed_grad = (
        dot_nt(middle_b, w_out).astype(jnp.bfloat16).reshape(img_group, TILE, heads_here, head_size)
    )
    prob_grad = jnp.einsum(
        "gqhd,gkhd->ghqk", mixed_grad, values_part, preferred_element_type=jnp.float32
    )
    score_grad = (
        probability
        * (prob_grad - jnp.sum(probability * prob_grad, axis=-1, keepdims=True))
        * scaling
    )
    score_grad = score_grad.astype(jnp.bfloat16)
    q_grad = jnp.einsum(
        "ghqk,gkhd->gqhd", score_grad, keys_part, preferred_element_type=jnp.float32
    )
    k_grad = jnp.einsum("ghqk,gqhd->gkhd", score_grad, queries, preferred_element_type=jnp.float32)
    v_grad = jnp.einsum("ghqk,gqhd->gkhd", prob_low, mixed_grad, preferred_element_type=jnp.float32)
    packed_grad = jnp.stack([q_grad, k_grad, v_grad], axis=3).astype(jnp.bfloat16)
    packed_grad = packed_grad.reshape(rows_here, heads_here * 3 * head_size)
    qkv_term = dot_tn(normed_in, packed_grad).reshape(features_dim, heads_here, 3 * head_size)
    in_part = dot_nt(packed_grad, qkv_flat)
    share_width = features_dim // lax.axis_size("tp")
    share_start = tp_rank * share_width
    in_share = summed_on_arrival(in_part.astype(jnp.bfloat16), "tp", 1)
    normed_share = lax.dynamic_slice_in_dim(normed1, share_start, share_width, 1)
    gain_share = lax.dynamic_slice_in_dim(ln1_gain, share_start, share_width, 0)
    scaled = in_share * gain_share
    plain_total, inner_total = in_one(
        (jnp.sum(scaled, axis=1), jnp.sum(scaled * normed_share, axis=1)), "tp"
    )
    in_back = inverse1 * (
        scaled
        - plain_total[:, None] / features_dim
        - normed_share * (inner_total[:, None] / features_dim)
    )
    ln1_term = gathered_copies(jnp.sum(in_share * normed_share, axis=0), "tp", 0)
    vis_share = lax.dynamic_slice_in_dim(vis_grad, share_start, share_width, 1)
    grad_input = (vis_share + in_back).astype(jnp.bfloat16)
    grad_qkv, grad_out, grad_ln1 = tuple(
        (
            part.astype(jnp.float32)
            for part in one_scatter(
                (
                    qkv_term.astype(jnp.bfloat16),
                    out_term.astype(jnp.bfloat16),
                    ln1_term.astype(jnp.bfloat16),
                ),
                ENC,
                (0, 1, 0),
            )
        )
    )
    return (grad_input, grad_proj, grad_qkv, grad_out, grad_ln1)


def solution(mesh):
    torus = Mesh(mesh.devices.reshape(8, 4, mesh.shape["tp"]), ("enc_0", "enc_1", "tp"))
    return jax.shard_map(
        shards,
        mesh=torus,
        in_specs=(
            P(ENC, "tp"),
            P(ENC, None),
            P(ENC, "tp"),
            P(),
            P(),
            P(),
            P(None, "tp", None),
            P("tp", None),
            P(None, "tp"),
        ),
        out_specs=(P(ENC, "tp"), P(ENC, "tp"), P(ENC, "tp", None), P("tp", ENC), P(ENC)),
        check_vma=False,
    )
```

profile of v0, /device:TPU:8, one launch (start us, length us, event | category | flops | bytes accessed | tf_op | source)
XLA Modules:
  0.0 435.3 jit_solution(17445175852899535516)
XLA Ops:
  9.7 4.4 %convolution_convert_fusion.1 = bf16[640,1280]{1,0:T(8,128)(2,1)} fusion(bf16[640,1024]{1,0:T(8,128)(2,1)} %param.11, bf16[1280,1024]{1,0:T(8,128)(2,1)S(1)} %copy-done), kind=kOutput, calls=%fused_computation.15 | convolution fusion | flops 1678540800 | bytes 5570560 | tf_op jit(solution)/shard_map/dot_general | solution.py:82
  14.2 3.5 copy.120
  17.7 6.5 %all-to-all-start = ((bf16[8,640,160]{1,2,0:T(8,128)(2,1)}), bf16[8,640,160]{1,2,0:T(8,128)(2,1)}, u32[]{:S(2)}, u32[]{:S(2)}) async-start(bf16[8,640,160]{1,2,0:T(8,128)(2,1)} %bitcast.114), calls=%async_computation | async-start | bytes 3276800 | tf_op jit(solution)/shard_map/all_to_all | solution.py:37
  24.5 20.6 %all-to-all-done = bf16[8,640,160]{1,2,0:T(8,128)(2,1)} async-done(((bf16[8,640,160]{1,2,0:T(8,128)(2,1)}), bf16[8,640,160]{1,2,0:T(8,128)(2,1)}, u32[]{:S(2)}, u32[]{:S(2)}) %all-to-all-start) | async-done | bytes 1638432 | tf_op jit(solution)/shard_map/all_to_all | solution.py:37
  53.1 3.0 convert_element_type.145
  56.1 10.1 %all-to-all-start.1 = ((bf16[32,128,160]{1,2,0:T(8,128)(2,1)}), bf16[32,128,160]{1,2,0:T(8,128)(2,1)}, u32[]{:S(2)}, u32[]{:S(2)}) async-start(bf16[32,128,160]{1,2,0:T(8,128)(2,1)} %convert_element_type.145), calls=%async_computation.1 | async-start | bytes 2621440 | tf_op jit(solution)/shard_map/all_to_all | solution.py:121
  66.8 32.7 %all-to-all-done.1 = bf16[32,128,160]{1,2,0:T(8,128)(2,1)} async-done(((bf16[32,128,160]{1,2,0:T(8,128)(2,1)}), bf16[32,128,160]{1,2,0:T(8,128)(2,1)}, u32[]{:S(2)}, u32[]{:S(2)}) %all-to-all-start.1) | async-done | bytes 1310752 | tf_op jit(solution)/shard_map/all_to_all | solution.py:121
  103.4 5.6 %all-to-all-start.2 = ((bf16[8,640,160]{1,2,0:T(8,128)(2,1)}), bf16[8,640,160]{1,2,0:T(8,128)(2,1)}, u32[]{:S(2)}, u32[]{:S(2)}) async-start(bf16[8,640,160]{1,2,0:T(8,128)(2,1)} %broadcast_in_dim.113), calls=%async_computation.2 | async-start | bytes 3276800 | tf_op jit(solution)/shard_map/all_to_all | solution.py:16
  109.1 5.8 %convolution_convert_fusion = bf16[1280,1024]{1,0:T(8,128)(2,1)} fusion(bf16[640,1024]{1,0:T(8,128)(2,1)} %param.11, bf16[640,1280]{1,0:T(8,128)(2,1)} %param.12, pred[640]{0:T(1024)(128)(4,1)S(1)} %get-tuple-element.39), kind=kOutput, calls=%fused_computation.6 | convolution fusion | flops 1679851520 | bytes 5571200 | tf_op jit(solution)/shard_map/dot_general | solution.py:88
  116.7 19.9 %all-to-all-done.2 = bf16[8,640,160]{1,2,0:T(8,128)(2,1)} async-done(((bf16[8,640,160]{1,2,0:T(8,128)(2,1)}), bf16[8,640,160]{1,2,0:T(8,128)(2,1)}, u32[]{:S(2)}, u32[]{:S(2)}) %all-to-all-start.2) | async-done | bytes 1638432 | tf_op jit(solution)/shard_map/all_to_all | solution.py:16
  156.5 2.9 convolution_bitcast_fusion.2
  164.5 3.5 copy.134
  168.0 5.6 %all-to-all-start.3 = ((bf16[8,640,160]{1,2,0:T(8,128)(2,1)}), bf16[8,640,160]{1,2,0:T(8,128)(2,1)}, u32[]{:S(2)}, u32[]{:S(2)}) async-start(bf16[8,640,160]{1,2,0:T(8,128)(2,1)} %bitcast.113), calls=%async_computation.3 | async-start | bytes 3276800 | tf_op jit(solution)/shard_map/all_to_all | solution.py:37
  175.9 3.4 convert_element_type.149
  179.4 3.6 convolution_convert_fusion.3
  183.0 11.6 %all-to-all-done.3 = bf16[8,640,160]{1,2,0:T(8,128)(2,1)} async-done(((bf16[8,640,160]{1,2,0:T(8,128)(2,1)}), bf16[8,640,160]{1,2,0:T(8,128)(2,1)}, u32[]{:S(2)}, u32[]{:S(2)}) %all-to-all-start.3) | async-done | bytes 1638432 | tf_op jit(solution)/shard_map/all_to_all | solution.py:37
  198.0 4.7 %all-to-all-start.5 = ((bf16[8,1,160]{2,1,0:T(2,128)(2,1)}), bf16[8,1,160]{2,1,0:T(2,128)(2,1)S(1)}, u32[]{:S(2)}, u32[]{:S(2)}) async-start(bf16[8,1,160]{2,1,0:T(2,128)(2,1)} %broadcast_in_dim.120), calls=%async_computation.7 | async-start | bytes 16384 | tf_op jit(solution)/shard_map/all_to_all | solution.py:16
  208.4 3.0 reshape.313
  211.4 4.3 copy.137
  215.7 4.0 reshape_reshape.3
  219.8 2.6 fusion.6
  222.5 2.9 reshape.314
  226.1 4.8 %all-to-all-start.4 = ((f32[8,1,1280]{2,1,0:T(1,128)}), f32[8,1,1280]{2,1,0:T(1,128)S(1)}, u32[]{:S(2)}, u32[]{:S(2)}) async-start(f32[8,1,1280]{2,1,0:T(1,128)} %broadcast_in_dim.117), calls=%async_computation.4 | async-start | bytes 81920 | tf_op jit(solution)/shard_map/all_to_all | solution.py:16
  236.9 186.5 %reduce-scatter.8.cloned.1.call-done = bf16[208,128]{1,0:T(8,128)(2,1)} async-done(((bf16[6656,128]{1,0:T(8,128)(2,1)}), bf16[208,128]{1,0:T(8,128)(2,1)}) %reduce-scatter.8.cloned.1.call-update) | async-done | bytes 53264 | tf_op jit(solution)/shard_map/reduce_scatter | solution.py:66
  (111 shorter events, 63.7 us)
Async XLA Ops:
  8.0 1.7 copy-start
  17.7 6.5 %copy-start.7 = (s32[32,5]{0,1:T(8,128)S(1)}, s32[32,5]{0,1:T(8,128)}, u32[]{:S(2)}) copy-start(s32[32,5]{0,1:T(8,128)} %param.15) | copy-start | bytes 1924
  17.7 6.5 %copy-start.8 = (s32[32,5]{0,1:T(8,128)S(1)}, s32[32,5]{0,1:T(8,128)}, u32[]{:S(2)}) copy-start(s32[32,5]{0,1:T(8,128)} %param.14) | copy-start | bytes 1924
  17.7 27.4 %all-to-all-start = ((bf16[8,640,160]{1,2,0:T(8,128)(2,1)}), bf16[8,640,160]{1,2,0:T(8,128)(2,1)}, u32[]{:S(2)}, u32[]{:S(2)}) async-start(bf16[8,640,160]{1,2,0:T(8,128)(2,1)} %bitcast.114), calls=%async_computation | async-start | bytes 3276800 | tf_op jit(solution)/shard_map/all_to_all | solution.py:37
  56.1 46.1 %copy-start.5 = (bf16[640,160]{0,1:T(8,128)(2,1)S(1)}, bf16[640,160]{0,1:T(8,128)(2,1)}, u32[]{:S(2)}) copy-start(bf16[640,160]{0,1:T(8,128)(2,1)} %param.13) | copy-start | bytes 614404
  56.1 43.4 %all-to-all-start.1 = ((bf16[32,128,160]{1,2,0:T(8,128)(2,1)}), bf16[32,128,160]{1,2,0:T(8,128)(2,1)}, u32[]{:S(2)}, u32[]{:S(2)}) async-start(bf16[32,128,160]{1,2,0:T(8,128)(2,1)} %convert_element_type.145), calls=%async_computation.1 | async-start | bytes 2621440 | tf_op jit(solution)/shard_map/all_to_all | solution.py:121
  66.2 84.6 %all-gather.2.cloned.1.call-start = ((), (), s32[]{:S(2)}) async-start(), calls=%async_computation.9 | async-start | bytes 1843200 | tf_op jit(solution)/shard_map/all_gather | solution.py:131
  103.4 33.2 %all-to-all-start.2 = ((bf16[8,640,160]{1,2,0:T(8,128)(2,1)}), bf16[8,640,160]{1,2,0:T(8,128)(2,1)}, u32[]{:S(2)}, u32[]{:S(2)}) async-start(bf16[8,640,160]{1,2,0:T(8,128)(2,1)} %broadcast_in_dim.113), calls=%async_computation.2 | async-start | bytes 3276800 | tf_op jit(solution)/shard_map/all_to_all | solution.py:16
  109.1 70.3 %reduce-scatter.4.cloned.1.call-start = ((), (), s32[]{:S(2)}) async-start(), calls=%async_computation.10 | async-start | bytes 2949120 | tf_op jit(solution)/shard_map/reduce_scatter | solution.py:44
  114.8 1.3 copy-start.9
  140.3 3.3 copy-start.10
  142.4 1.2 copy-start.1
  148.4 2.4 copy-start.4
  159.3 1.5 copy-start.6
  160.9 1.3 copy-start.11
  161.4 0.8 copy-start.2
  168.0 26.6 %all-to-all-start.3 = ((bf16[8,640,160]{1,2,0:T(8,128)(2,1)}), bf16[8,640,160]{1,2,0:T(8,128)(2,1)}, u32[]{:S(2)}, u32[]{:S(2)}) async-start(bf16[8,640,160]{1,2,0:T(8,128)(2,1)} %bitcast.113), calls=%async_computation.3 | async-start | bytes 3276800 | tf_op jit(solution)/shard_map/all_to_all | solution.py:37
  173.6 57.3 %reduce-scatter.6.cloned.1.call-start = ((), (), s32[]{:S(2)}) async-start(), calls=%async_computation.11 | async-start | bytes 409600 | tf_op jit(solution)/shard_map/reduce_scatter | solution.py:44
  175.9 3.5 copy-start.3
  198.0 21.7 %all-to-all-start.5 = ((bf16[8,1,160]{2,1,0:T(2,128)(2,1)}), bf16[8,1,160]{2,1,0:T(2,128)(2,1)S(1)}, u32[]{:S(2)}, u32[]{:S(2)}) async-start(bf16[8,1,160]{2,1,0:T(2,128)(2,1)} %broadcast_in_dim.120), calls=%async_computation.7 | async-start | bytes 16384 | tf_op jit(solution)/shard_map/all_to_all | solution.py:16
  202.7 220.7 %reduce-scatter.8.cloned.1.call-start = ((), (), s32[]{:S(2)}) async-start(), calls=%async_computation.12 | async-start | bytes 1757184 | tf_op jit(solution)/shard_map/reduce_scatter | solution.py:66
  226.1 8.8 %all-to-all-start.4 = ((f32[8,1,1280]{2,1,0:T(1,128)}), f32[8,1,1280]{2,1,0:T(1,128)S(1)}, u32[]{:S(2)}, u32[]{:S(2)}) async-start(f32[8,1,1280]{2,1,0:T(1,128)} %broadcast_in_dim.117), calls=%async_computation.4 | async-start | bytes 81920 | tf_op jit(solution)/shard_map/all_to_all | solution.py:16
Sparse Core Ops, SparseCore 0:
  102.2 27.0 all-gather.1
Sparse Core Ops, SparseCore 1:
  114.9 41.0 reduce-scatter.3
  179.4 20.7 reduce-scatter.5
  225.5 197.8 reduce-scatter.7
where the time goes:
time: 437 us; the launch traced here: 435 us
  waiting for transfers between devices  274 us (63%)
  local copies, waits for them, and re-layouts  47.3 us (11%)
  starting transfers between devices  37.4 us (9%)
  matrix products  32.8 us (8%)
  other arithmetic  28.1 us (6%)
  between operations  15.9 us (4%)
    reduce_scatter x1, waiting for transfers between devices, one_scatter(): lax.psum_scatter(lines, axis, tiled=True).reshape(-1)  186 us
    all_to_all x1, waiting for transfers between devices, shards(): lax.all_to_all(jnp.zeros((groups, TILE, columns), shared.dtype).at[own_ow...  32.7 us
    all_to_all x2, waiting for transfers between devices, summed_on_arrival(): lax.all_to_all(blocks, axis, split_axis=0, concat_axis=0, tiled=True)  32.2 us
    all_to_all x3, waiting for transfers between devices, from_everyone(): return lax.all_to_all(copies, axis, split_axis=0, concat_axis=0, tiled=True)  22.4 us
    all_to_all x3, starting transfers between devices, from_everyone(): return lax.all_to_all(copies, axis, split_axis=0, concat_axis=0, tiled=True)  15.1 us
    all_to_all x2, starting transfers between devices, summed_on_arrival(): lax.all_to_all(blocks, axis, split_axis=0, concat_axis=0, tiled=True)  12.1 us
    dot_general x3, matrix products, dot_tn(): lax.dot_general(left, right, (((0,), (0,)), ((), ())), preferred_element_...  11.6 us
    all_to_all x1, starting transfers between devices, shards(): lax.all_to_all(jnp.zeros((groups, TILE, columns), shared.dtype).at[own_ow...  10.1 us
  transfers between devices with their start and end apart: 10, of which 6 were waited for; matrix products, arithmetic and copies ran while one was open for 18% of the time, Pallas kernels for 0%

commit v1 on v0

v1 whole, which is shorter than its diff:
```python
import jax
import jax.numpy as jnp
from jax import lax
from jax.experimental import pallas as pl
from jax.experimental.pallas import tpu as pltpu
from jax.sharding import Mesh
from jax.sharding import PartitionSpec as P

TILE = 128
IMG = 5
ROWS = IMG * TILE
WIDTH = 1280
HEAD = 80
LANE = 128
PEERS = 32
ENC = ("z", "x")
TP = ("y", "c")
EPSILON = 1e-05
SCALING = 1.0 / HEAD**0.5
BF = jnp.bfloat16
F32 = jnp.float32
SWAP = ((0, 1), (1, 0))


def exchanged(blocks, axis):
    return lax.all_to_all(blocks, axis, split_axis=0, concat_axis=0, tiled=True)


def dot(left, right, dim_left, dim_right):
    return lax.dot_general(
        left, right, (((dim_left,), (dim_right,)), ((), ())), preferred_element_type=F32
    )


def smem():
    return pl.BlockSpec(memory_space=pltpu.SMEM)


def normalize(values):
    centred = values - jnp.mean(values, axis=-1, keepdims=True)
    variance = jnp.mean(centred * centred, axis=-1, keepdims=True)
    inverse = lax.rsqrt(variance + EPSILON)
    return (centred * inverse, inverse)


def shifted_sum(pieces, lanes):
    total = None
    for at, piece in enumerate(pieces):
        wide = jnp.concatenate(
            [piece, jnp.zeros((piece.shape[0], lanes - LANE), piece.dtype)], axis=1
        )
        if at:
            wide = pltpu.roll(wide, HEAD * at, 1)
        total = wide if total is None else total + wide
    return total


def spread_kernel(place_ref, counts_ref, arrived_ref, out_ref):
    first_row = place_ref[0] * 16
    for image in range(IMG):
        rows = arrived_ref[0, image].astype(F32)
        for peer in range(1, 4):
            rows = rows + arrived_ref[peer, image].astype(F32)
        line = first_row + lax.broadcasted_iota(jnp.int32, rows.shape, 0)
        rows = jnp.where(line < counts_ref[image], rows, 0.0).astype(BF)
        for half in range(2):
            for group in range(10):
                out_ref[half * 10 + group, image] = rows[
                    half * 8 : half * 8 + 8, group * LANE : (group + 1) * LANE
                ]
    out_ref[20:32] = jnp.zeros((12, IMG, 8, LANE), BF)


def spread(place, counts, arrived):
    return pl.pallas_call(
        spread_kernel,
        out_shape=jax.ShapeDtypeStruct((PEERS, IMG, 8, LANE), BF),
        in_specs=[smem(), smem(), pl.BlockSpec(memory_space=pltpu.VMEM)],
        out_specs=pl.BlockSpec(memory_space=pltpu.VMEM),
        name="spread",
    )(place, counts, arrived)


def forward_kernel(index_ref, pieces_ref, out_ref):
    def step(at, carry):
        out_ref[at] = pieces_ref[index_ref[at]]
        return carry

    lax.fori_loop(0, PEERS * IMG, step, 0, unroll=8)


def forwarded(index, pieces):
    flat = pieces.reshape(PEERS * IMG, 8, LANE)
    return pl.pallas_call(
        forward_kernel,
        out_shape=jax.ShapeDtypeStruct(flat.shape, BF),
        in_specs=[smem(), pl.BlockSpec(memory_space=pltpu.VMEM)],
        out_specs=pl.BlockSpec(memory_space=pltpu.VMEM),
        name="forwarded",
    )(index, flat).reshape(pieces.shape)


def collect_kernel(pieces_ref, rows_ref, copies_ref):
    for image in range(IMG):
        for half in range(2):
            for group in range(10):
                piece = pieces_ref[half * 10 + group, image]
                at = (slice(half * 8, half * 8 + 8), slice(group * LANE, (group + 1) * LANE))
                rows_ref[image, at[0], at[1]] = piece
                for peer in range(4):
                    copies_ref[peer, image, at[0], at[1]] = piece


def collected(pieces):
    return pl.pallas_call(
        collect_kernel,
        out_shape=(
            jax.ShapeDtypeStruct((IMG, 16, WIDTH), BF),
            jax.ShapeDtypeStruct((4, IMG, 16, WIDTH), BF),
        ),
        in_specs=[pl.BlockSpec(memory_space=pltpu.VMEM)],
        out_specs=(pl.BlockSpec(memory_space=pltpu.VMEM),) * 2,
        name="collected",
    )(pieces)


def attention_kernel(
    counts_ref, block_ref, gain_ref, w_ref, normed_ref, packed_ref, prob_ref, mixed_ref
):
    normed, _ = normalize(block_ref[...].astype(F32))
    normed_in = (normed * gain_ref[...]).astype(BF)
    normed_ref[...] = normed_in
    packed = dot(normed_in, w_ref[...], 1, 0).astype(BF)
    packed_ref[...] = packed
    count = counts_ref[pl.program_id(0)]
    live_row = lax.broadcasted_iota(jnp.int32, (TILE, TILE), 0) < count
    live_col = lax.broadcasted_iota(jnp.int32, (TILE, TILE), 1) < count
    same_kind = (live_row & live_col) | (~live_row & ~live_col)
    mixed = []
    for head in range(2):
        query, key, value = (
            packed[:, (head * 3 + i) * LANE : (head * 3 + i + 1) * LANE] for i in range(3)
        )
        scores = jnp.where(same_kind, dot(query, key, 1, 1) * SCALING, -1e30)
        exp_terms = jnp.exp(scores - jnp.max(scores, axis=-1, keepdims=True))
        probability = exp_terms / jnp.sum(exp_terms, axis=-1, keepdims=True)
        prob_ref[0, head] = probability
        mixed.append(dot(probability.astype(BF), value, 1, 0))
    mixed_ref[...] = shifted_sum(mixed, 256)[:, :160].astype(BF)


def attention(counts, block, gain, w_pad):
    return pl.pallas_call(
        attention_kernel,
        grid=(IMG,),
        out_shape=(
            jax.ShapeDtypeStruct((ROWS, WIDTH), BF),
            jax.ShapeDtypeStruct((ROWS, 6 * LANE), BF),
            jax.ShapeDtypeStruct((IMG, 2, TILE, TILE), F32),
            jax.ShapeDtypeStruct((ROWS, 2 * HEAD), BF),
        ),
        in_specs=[
            smem(),
            pl.BlockSpec((TILE, WIDTH), lambda i: (i, 0)),
            pl.BlockSpec((1, WIDTH), lambda i: (0, 0)),
            pl.BlockSpec((WIDTH, 6 * LANE), lambda i: (0, 0)),
        ],
        out_specs=(
            pl.BlockSpec((TILE, WIDTH), lambda i: (i, 0)),
            pl.BlockSpec((TILE, 6 * LANE), lambda i: (i, 0)),
            pl.BlockSpec((1, 2, TILE, TILE), lambda i: (i, 0, 0, 0)),
            pl.BlockSpec((TILE, 2 * HEAD), lambda i: (i, 0)),
        ),
        name="attention",
    )(counts, block, gain, w_pad)


def backward_kernel(
    core_ref,
    own_ref,
    other_ref,
    wout_ref,
    w_ref,
    packed_ref,
    prob_ref,
    upstream_ref,
    packed_grad_ref,
    in_own_ref,
    in_other_ref,
):
    first = core_ref[0] == 0
    own = own_ref[...].reshape(64, WIDTH)
    other = other_ref[...].reshape(64, WIDTH)
    upstream = jnp.concatenate(
        [jnp.where(first, own, other), jnp.where(first, other, own)], axis=0
    )
    upstream_ref[...] = upstream
    mixed_grads = dot(upstream, wout_ref[...], 1, 1).astype(BF)
    pieces = []
    for head in range(2):
        query, key, value = (
            packed_ref[:, (head * 3 + i) * LANE : (head * 3 + i + 1) * LANE] for i in range(3)
        )
        probability = prob_ref[0, head]
        mixed_grad = mixed_grads[:, head * LANE : (head + 1) * LANE]
        prob_grad = dot(mixed_grad, value, 1, 1)
        inner = jnp.sum(probability * prob_grad, axis=-1, keepdims=True)
        score_grad = (probability * (prob_grad - inner) * SCALING).astype(BF)
        pieces.append(dot(score_grad, key, 1, 0))
        pieces.append(dot(score_grad, query, 0, 0))
        pieces.append(dot(probability.astype(BF), mixed_grad, 0, 0))
    packed_grad_ref[...] = shifted_sum(pieces, 512)[:, :480].astype(BF)
    wide = jnp.concatenate([piece.astype(BF) for piece in pieces], axis=1)
    in_part = dot(wide, w_ref[...], 1, 1).astype(BF)
    low, high = in_part[:64], in_part[64:]
    in_own_ref[...] = jnp.where(first, low, high).reshape(4, 1, 16, WIDTH)
    in_other_ref[...] = jnp.where(first, high, low).reshape(4, 1, 16, WIDTH)


def backward(core, own, other, wout_pad, w_pad, packed, prob):
    quarter = pl.BlockSpec((4, 1, 16, WIDTH), lambda i: (0, i, 0, 0))
    return pl.pallas_call(
        backward_kernel,
        grid=(IMG,),
        out_shape=(
            jax.ShapeDtypeStruct((ROWS, WIDTH), BF),
            jax.ShapeDtypeStruct((ROWS, 6 * HEAD), BF),
            jax.ShapeDtypeStruct((4, IMG, 16, WIDTH), BF),
            jax.ShapeDtypeStruct((4, IMG, 16, WIDTH), BF),
        ),
        in_specs=[
            smem(),
            quarter,
            quarter,
            pl.BlockSpec((2 * LANE, WIDTH), lambda i: (0, 0)),
            pl.BlockSpec((WIDTH, 6 * LANE), lambda i: (0, 0)),
            pl.BlockSpec((TILE, 6 * LANE), lambda i: (i, 0)),
            pl.BlockSpec((1, 2, TILE, TILE), lambda i: (i, 0, 0, 0)),
        ],
        out_specs=(
            pl.BlockSpec((TILE, WIDTH), lambda i: (i, 0)),
            pl.BlockSpec((TILE, 6 * HEAD), lambda i: (i, 0)),
            quarter,
            quarter,
        ),
        name="backward",
    )(core, own, other, wout_pad, w_pad, packed, prob)


def weights_kernel(normed_ref, upstream_ref, packed_grad_ref, mixed_ref, out_ref):
    qkv = dot(normed_ref[...], packed_grad_ref[...], 0, 0)
    out = dot(upstream_ref[...], mixed_ref[...], 0, 0)
    term = jnp.concatenate([qkv, out], axis=1).astype(BF)
    for far in range(4):
        for near in range(4):
            at = (far * 4 + near) * 40
            out_ref[near, far] = term[at : at + 40]


def weight_terms(normed, upstream, packed_grad, mixed):
    return pl.pallas_call(
        weights_kernel,
        grid=(2,),
        out_shape=jax.ShapeDtypeStruct((4, 8, 40, 640), BF),
        in_specs=[
            pl.BlockSpec((ROWS, 640), lambda i: (0, i)),
            pl.BlockSpec((ROWS, 640), lambda i: (0, i)),
            pl.BlockSpec((ROWS, 6 * HEAD), lambda i: (0, 0)),
            pl.BlockSpec((ROWS, 2 * HEAD), lambda i: (0, 0)),
        ],
        out_specs=pl.BlockSpec((4, 4, 40, 640), lambda i: (0, i, 0, 0)),
        name="weight_terms",
    )(normed, upstream, packed_grad, mixed)


def norm_back_kernel(arrived_ref, block_ref, upstream_ref, gain_ref, out_ref):
    gain = gain_ref[...]
    gain_term = None
    results = []
    for image in range(IMG):
        incoming = arrived_ref[0, image].astype(F32)
        for peer in range(1, 4):
            incoming = incoming + arrived_ref[peer, image].astype(F32)
        normed, inverse = normalize(block_ref[image].astype(F32))
        term = jnp.sum(incoming * normed, axis=0, keepdims=True)
        gain_term = term if gain_term is None else gain_term + term
        scaled = incoming * gain
        inner = jnp.mean(scaled * normed, axis=-1, keepdims=True)
        outgoing = inverse * (scaled - jnp.mean(scaled, axis=-1, keepdims=True) - normed * inner)
        results.append(upstream_ref[image].astype(F32) + outgoing)
    grads = jnp.concatenate(results, axis=0)
    spread_term = jnp.broadcast_to(gain_term, (8, WIDTH))
    row = lax.broadcasted_iota(jnp.int32, (8, 160), 0)
    terms = jnp.zeros((8, 160), F32)
    for share in range(8):
        start = share * 160 // LANE * LANE
        offset = share * 160 - start
        lanes = 256 if offset + 160 <= 256 else 384
        lanes = min(lanes, WIDTH - start)

        def part(values):
            window = values[:, start : start + lanes]
            if offset:
                window = pltpu.roll(window, lanes - offset, 1)
            return window[:, :160]

        out_ref[share, 0:80] = part(grads).astype(BF)
        terms = jnp.where(row == share, part(spread_term), terms)
    for share in range(8):
        out_ref[share, 80:88] = terms.astype(BF)


def norm_back(arrived, block_rows, upstream_rows, gain):
    return pl.pallas_call(
        norm_back_kernel,
        out_shape=jax.ShapeDtypeStruct((8, 88, 160), BF),
        in_specs=[pl.BlockSpec(memory_space=pltpu.VMEM)] * 4,
        out_specs=pl.BlockSpec(memory_space=pltpu.VMEM),
        name="norm_back",
    )(arrived, block_rows, upstream_rows, gain)


def summed(blocks):
    return blocks.astype(F32).sum(axis=0)


def shards(grad_rows, features, block_in, patch_counts, owner, ln1_gain, w_qkv, w_out, w_proj):
    device = lax.axis_index(ENC)
    core = lax.axis_index("c")
    place = core * 4 + lax.axis_index("y")
    core_word = core.reshape(1).astype(jnp.int32)
    place_word = place.reshape(1).astype(jnp.int32)
    gain = ln1_gain.reshape(1, WIDTH)

    own_counts = lax.dynamic_index_in_dim(patch_counts, device, 0, keepdims=False)
    images = jnp.arange(PEERS * IMG, dtype=jnp.int32)
    block_of = images // IMG
    owners = owner.reshape(-1)
    ahead = (owners[:, None] == owners[None, :]) & (block_of[None, :] < block_of[:, None])
    target = owners * IMG + jnp.sum(ahead.astype(jnp.int32), axis=1)
    hits = target[None, :] == images[:, None]
    source_of = jnp.sum(jnp.where(hits, images[None, :], 0), axis=1)
    all_counts = jnp.sum(jnp.where(hits, patch_counts.reshape(1, -1), 0), axis=1)
    arrived_counts = lax.dynamic_slice_in_dim(all_counts, device * IMG, IMG, 0)

    by_place = grad_rows.reshape(IMG, 2, 4, 16, -1).transpose(1, 2, 0, 3, 4)
    by_place = by_place.reshape(2, ROWS // 2, -1)
    for_other = lax.dynamic_index_in_dim(by_place, 1 - core, 0, keepdims=False)
    for_own = lax.dynamic_index_in_dim(by_place, core, 0, keepdims=False)
    part_other = dot(for_other, w_proj, 1, 1).astype(BF)
    from_other = lax.ppermute(part_other, "c", SWAP)
    part_own = dot(for_own, w_proj, 1, 1)
    pair = (part_own + from_other.astype(F32)).astype(BF)
    arrived = exchanged(pair.reshape(4, 80, WIDTH), "y").reshape(4, IMG, 16, WIDTH)
    pieces = spread(place_word, own_counts, arrived)

    passing = exchanged(pieces, ENC)
    passing = forwarded(source_of, passing)
    landed = exchanged(passing, ENC)
    upstream_rows, copies = collected(landed)
    half_own = exchanged(copies.reshape(4, 80, WIDTH), "y").reshape(4, IMG, 16, WIDTH)
    half_other = lax.ppermute(half_own, "c", SWAP)

    line = jnp.arange(TILE, dtype=jnp.int32)
    live_own = (line[None, :] < own_counts[:, None]).reshape(-1)
    kept_rows = jnp.where(live_own[:, None], features, jnp.zeros_like(features))
    proj_term = dot(kept_rows, grad_rows, 0, 0).astype(BF)
    columns = grad_rows.shape[1]
    proj_term = proj_term.reshape(8, 4, 40, columns).transpose(1, 0, 2, 3)
    proj_near = summed(exchanged(proj_term.reshape(4, 320, columns), "x")).astype(BF)
    grad_proj = summed(exchanged(proj_near.reshape(8, 40, columns), "z"))

    lines = block_in.reshape(ROWS * 160 // LANE, LANE)
    lines, pieces = lax.optimization_barrier((lines, pieces))
    lines_own = exchanged(jnp.broadcast_to(lines, (4, *lines.shape)), "y")
    lines_other = lax.ppermute(lines_own, "c", SWAP)
    first = core == 0
    both = jnp.stack(
        [jnp.where(first, lines_own, lines_other), jnp.where(first, lines_other, lines_own)], 1
    )
    block_full = both.reshape(8, ROWS, 160).transpose(1, 0, 2).reshape(ROWS, WIDTH)
    block_rows = lax.dynamic_index_in_dim(
        block_full.reshape(IMG, 8, 16, WIDTH), place, 1, keepdims=False
    )

    w_pad = jnp.pad(w_qkv.reshape(WIDTH, 6, HEAD), ((0, 0), (0, 0), (0, LANE - HEAD)))
    w_pad = w_pad.reshape(WIDTH, 6 * LANE)
    wout_pad = jnp.pad(w_out.reshape(2, HEAD, WIDTH), ((0, 0), (0, LANE - HEAD), (0, 0)))
    wout_pad = wout_pad.reshape(2 * LANE, WIDTH)
    normed_in, packed, prob, mixed = attention(arrived_counts, block_full, gain, w_pad)

    upstream, packed_grad, in_own, in_other = backward(
        core_word, half_own, half_other, wout_pad, w_pad, packed, prob
    )
    in_got = lax.ppermute(in_other, "c", SWAP)
    terms = weight_terms(normed_in, upstream, packed_grad, mixed)
    in_pair = (in_own.astype(F32) + in_got.astype(F32)).astype(BF)
    in_arrived = exchanged(in_pair.reshape(4, 80, WIDTH), "y").reshape(4, IMG, 16, WIDTH)
    term_near = summed(exchanged(terms.reshape(4, 320, 640), "x")).astype(BF)
    shares = exchanged(norm_back(in_arrived, block_rows, upstream_rows, gain), TP)
    grad_input = shares[:, :80].reshape(4, 2, IMG, 16, 160).transpose(2, 1, 0, 3, 4)
    grad_input = grad_input.reshape(ROWS, 160)
    ln1_block = summed(shares[:, 80:]).astype(BF)
    grad_ln1 = summed(exchanged(ln1_block.reshape(PEERS, 1, 40), ENC)).reshape(40)
    term_sum = summed(exchanged(term_near.reshape(8, 40, 640), "z"))
    grad_qkv = term_sum[:, :480].reshape(40, 2, 240)
    grad_out = term_sum[:, 480:].T
    return (grad_input, grad_proj, grad_qkv, grad_out, grad_ln1)


def solution(mesh):
    torus = Mesh(mesh.devices.reshape(8, 4, 4, 2), ("z", "x", "y", "c"))
    return jax.shard_map(
        shards,
        mesh=torus,
        in_specs=(
            P(ENC, TP),
            P(ENC, None),
            P(ENC, TP),
            P(),
            P(),
            P(),
            P(None, TP, None),
            P(TP, None),
            P(None, TP),
        ),
        out_specs=(P(ENC, TP), P(ENC, TP), P(ENC, TP, None), P(TP, ENC), P(ENC)),
        check_vma=False,
    )
```

time: 437 us -> 280 us (0.64)
  waiting for transfers between devices: 274 us -> 104 us
  Pallas kernels: 0 us -> 34.8 us
  starting transfers between devices: 37.4 us -> 61.8 us
  matrix products: 32.8 us -> 10.5 us
  between operations: 15.9 us -> 0.81 us
  other arithmetic: 28.1 us -> 14.6 us
    reduce_scatter x3 -> x0, waiting for transfers between devices: 186 us -> none  [the longest x1 186 us: one_scatter(): lax.psum_scatter(lines, axis, tiled=True).reshape(-1)]
    pallas_call x0 -> x7, Pallas kernels: none -> 34.8 us  [the longest x1 12.3 us: backward(): pl.pallas_call(backward_kernel, grid=(IMG,), out_shape=(jax.ShapeDtypeStr...]
    all_to_all x6 -> x12, starting transfers between devices: 37.4 us -> 61.5 us  [exchanged(): return lax.all_to_all(blocks, axis, split_axis=0, concat_axis=0, tiled=True)]
    dot_general x12 -> x3, matrix products: 30.5 us -> 10.5 us  [dot(): lax.dot_general(left, right, (((dim_left,), (dim_right,)), ((), ())), pre...]
    convert_element_type x11 -> x0, local copies, waits for them, and re-layouts: 14.8 us -> none  [the longest x1 4.33 us: shards(): qkv_term.astype(jnp.bfloat16)]
    convert_element_type x11 -> x1, other arithmetic: 15.4 us -> 2.31 us  [shards(): in_pair = (in_own.astype(F32) + in_got.astype(F32)).astype(BF)]
    all_to_all x6 -> x12, waiting for transfers between devices: 87.2 us -> 99.1 us  [exchanged(): return lax.all_to_all(blocks, axis, split_axis=0, concat_axis=0, tiled=True)]
    transpose x1 -> x5, local copies, waits for them, and re-layouts: 2.33 us -> 13.3 us  [the longest x2 8.86 us: shards(): both.reshape(8, ROWS, 160).transpose(1, 0, 2).reshape(ROWS, WIDTH)]
  transfers between devices with their start and end apart: 10 -> 16, of which waited for: 6 -> 13; matrix products, arithmetic and copies ran while one was open for 18% -> 22% of each run, Pallas kernels for 0% -> 11%
where the time goes in v1:
time: 280 us; the launch traced here: 277 us
  waiting for transfers between devices  104 us (37%)
  starting transfers between devices  61.8 us (22%)
  local copies, waits for them, and re-layouts  51 us (18%)
  Pallas kernels  34.8 us (12%)
  other arithmetic  14.6 us (5%)
  matrix products  10.5 us (4%)
    all_to_all x12, waiting for transfers between devices, exchanged(): return lax.all_to_all(blocks, axis, split_axis=0, concat_axis=0, tiled=True)  99.1 us
    all_to_all x12, starting transfers between devices, exchanged(): return lax.all_to_all(blocks, axis, split_axis=0, concat_axis=0, tiled=True)  61.5 us
    pallas_call x1, Pallas kernels, backward(): pl.pallas_call(backward_kernel, grid=(IMG,), out_shape=(jax.ShapeDtypeStr...  12.3 us
    dot_general x3, matrix products, dot(): lax.dot_general(left, right, (((dim_left,), (dim_right,)), ((), ())), pre...  10.5 us
    pallas_call x1, Pallas kernels, attention(): pl.pallas_call(attention_kernel, grid=(IMG,), out_shape=(jax.ShapeDtypeSt...  9.16 us
    transpose x2, local copies, waits for them, and re-layouts, shards(): both.reshape(8, ROWS, 160).transpose(1, 0, 2).reshape(ROWS, WIDTH)  8.86 us
    reshape x2, local copies, waits for them, and re-layouts, shards(): both.reshape(8, ROWS, 160).transpose(1, 0, 2).reshape(ROWS, WIDTH)  8.64 us
    reduce_sum x6, other arithmetic, summed(): return blocks.astype(F32).sum(axis=0)  8.5 us
  transfers between devices with their start and end apart: 16, of which 13 were waited for; matrix products, arithmetic and copies ran while one was open for 22% of the time, Pallas kernels for 11%

profile of v1, /device:TPU:8, one launch (start us, length us, event | category | flops | bytes accessed | tf_op | source)
XLA Modules:
  0.0 277.5 jit_solution(17821415442235400447)
XLA Ops:
  12.0 5.8 %all-to-all-start = ((bf16[4,80,1280]{2,1,0:T(8,128)(2,1)}), bf16[4,80,1280]{2,1,0:T(8,128)(2,1)S(1)}, u32[]{:S(2)}, u32[]{:S(2)}) async-start(bf16[4,80,1280]{2,1,0:T(8,128)(2,1)} %bitcast.80), calls=%async_computation | async-start | bytes 1638400 | tf_op jit(solution)/shard_map/all_to_all | solution.py:26
  18.5 11.1 %all-to-all-done = bf16[4,80,1280]{2,1,0:T(8,128)(2,1)S(1)} async-done(((bf16[4,80,1280]{2,1,0:T(8,128)(2,1)}), bf16[4,80,1280]{2,1,0:T(8,128)(2,1)S(1)}, u32[]{:S(2)}, u32[]{:S(2)}) %all-to-all-start) | async-done | bytes 819232 | tf_op jit(solution)/shard_map/all_to_all | solution.py:26
  32.4 10.5 %all-to-all-start.1 = ((bf16[32,5,8,128]{3,2,1,0:T(8,128)(2,1)}), bf16[32,5,8,128]{3,2,1,0:T(8,128)(2,1)S(1)}, u32[]{:S(2)}, u32[]{:S(2)}) async-start(bf16[32,5,8,128]{3,2,1,0:T(8,128)(2,1)} %spread.1), calls=%async_computation.1 | async-start | bytes 655360 | tf_op jit(solution)/shard_map/all_to_all | solution.py:26
  44.3 12.1 %all-to-all-done.1 = bf16[32,5,8,128]{3,2,1,0:T(8,128)(2,1)S(1)} async-done(((bf16[32,5,8,128]{3,2,1,0:T(8,128)(2,1)}), bf16[32,5,8,128]{3,2,1,0:T(8,128)(2,1)S(1)}, u32[]{:S(2)}, u32[]{:S(2)}) %all-to-all-start.1) | async-done | bytes 327712 | tf_op jit(solution)/shard_map/all_to_all | solution.py:26
  63.7 12.5 %all-to-all-done.2.pieces_ref = bf16[32,5,8,128]{3,2,1,0:T(8,128)(2,1)S(1)} async-done(((bf16[32,5,8,128]{3,2,1,0:T(8,128)(2,1)}), bf16[32,5,8,128]{3,2,1,0:T(8,128)(2,1)S(1)}, u32[]{:S(2)}, u32[]{:S(2)}) %all-to-all-start.2) | async-done | bytes 327712 | tf_op jit(solution)/shard_map/all_to_all | solution.py:26
  77.3 5.1 %all-to-all-start.4 = ((bf16[4,800,128]{2,1,0:T(8,128)(2,1)}), bf16[4,800,128]{2,1,0:T(8,128)(2,1)S(1)}, u32[]{:S(2)}, u32[]{:S(2)}) async-start(bf16[4,800,128]{2,1,0:T(8,128)(2,1)} %broadcast_in_dim.45), calls=%async_computation.4 | async-start | bytes 1638400 | tf_op jit(solution)/shard_map/all_to_all | solution.py:26
  84.4 6.1 %all-to-all-done.4 = bf16[4,800,128]{2,1,0:T(8,128)(2,1)S(1)} async-done(((bf16[4,800,128]{2,1,0:T(8,128)(2,1)}), bf16[4,800,128]{2,1,0:T(8,128)(2,1)S(1)}, u32[]{:S(2)}, u32[]{:S(2)}) %all-to-all-start.4) | async-done | bytes 819232 | tf_op jit(solution)/shard_map/all_to_all | solution.py:26
  91.4 4.9 %all-to-all-start.3 = ((bf16[4,80,1280]{2,1,0:T(8,128)(2,1)}), bf16[4,80,1280]{2,1,0:T(8,128)(2,1)S(1)}, u32[]{:S(2)}, u32[]{:S(2)}) async-start(bf16[4,80,1280]{2,1,0:T(8,128)(2,1)} %bitcast.81), calls=%async_computation.3 | async-start | bytes 1638400 | tf_op jit(solution)/shard_map/all_to_all | solution.py:26
  96.4 8.1 %all-to-all-done.3 = bf16[4,80,1280]{2,1,0:T(8,128)(2,1)S(1)} async-done(((bf16[4,80,1280]{2,1,0:T(8,128)(2,1)}), bf16[4,80,1280]{2,1,0:T(8,128)(2,1)S(1)}, u32[]{:S(2)}, u32[]{:S(2)}) %all-to-all-start.3) | async-done | bytes 819232 | tf_op jit(solution)/shard_map/all_to_all | solution.py:26
  104.6 4.4 %convolution_convert_fusion = bf16[1280,1024]{1,0:T(8,128)(2,1)S(1)} fusion(bf16[640,1024]{1,0:T(8,128)(2,1)} %param.9, bf16[640,1280]{1,0:T(8,128)(2,1)} %param.10, pred[640]{0:T(1024)(128)(4,1)S(1)} %fusion.10), kind=kOutput, calls=%fused_computation | convolution fusion | flops 1679851520 | bytes 5571200 | tf_op jit(solution)/shard_map/dot_general | solution.py:30
  110.8 4.9 %all-to-all-start.7 = ((bf16[4,320,1024]{2,1,0:T(8,128)(2,1)}), bf16[4,320,1024]{2,1,0:T(8,128)(2,1)}, u32[]{:S(2)}, u32[]{:S(2)}) async-start(bf16[4,320,1024]{2,1,0:T(8,128)(2,1)} %bitcast.59), calls=%async_computation.7 | async-start | bytes 5242880 | tf_op jit(solution)/shard_map/all_to_all | solution.py:26
  128.4 5.1 %reshape.173 = bf16[8,640,160]{2,1,0:T(8,128)(2,1)} reshape(bf16[4,2,800,128]{3,2,1,0:T(8,128)(2,1)} %pad_maximum_fusion) | data formatting | bytes 3276800 | tf_op jit(solution)/shard_map/reshape | solution.py:381
  141.2 9.2 %attention.1 = (bf16[640,1280]{1,0:T(8,128)(2,1)}, bf16[640,768]{1,0:T(8,128)(2,1)}, f32[5,2,128,128]{3,2,1,0:T(8,128)}, bf16[640,160]{1,0:T(8,128)(2,1)}) custom-call(s32[5]{0:T(128)} %dynamic_slice.21.counts_ref, bf16[640,1280]{1,0:T(8,128)(2,1)} %copy.94.block_ref, f32[1,1280]{1,0:T(1,128)} %reshape.175.gain_ref, bf16[1280,768]{1,0:T(8,128)(2,1)} %copy.96.w_ref), custom_call_target="tpu_custom_call" | custom-call | tf_op jit(solution)/shard_map/attention/pallas_call | solution.py:153
  150.3 12.3 %backward.1 = (bf16[640,1280]{1,0:T(8,128)(2,1)}, bf16[640,480]{1,0:T(8,128)(2,1)}, bf16[4,5,16,1280]{3,2,1,0:T(8,128)(2,1)}, bf16[4,5,16,1280]{3,2,1,0:T(8,128)(2,1)}) custom-call(s32[1]{0:T(128)} %bitcast.core_ref, bf16[4,5,16,1280]{3,2,1,0:T(8,128)(2,1)} %bitcast.64, bf16[4,5,16,1280]{3,2,1,0:T(8,128)(2,1)} %collective-permute-done.1.other_ref, ...), custom_call_target="tpu_custom_call" | custom-call | tf_op jit(solution)/shard_map/backward/pallas_call | solution.py:222
  167.6 4.9 %all-to-all-start.5 = ((bf16[4,80,1280]{2,1,0:T(8,128)(2,1)}), bf16[4,80,1280]{2,1,0:T(8,128)(2,1)S(1)}, u32[]{:S(2)}, u32[]{:S(2)}) async-start(bf16[4,80,1280]{2,1,0:T(8,128)(2,1)} %bitcast.22), calls=%async_computation.5 | async-start | bytes 1638400 | tf_op jit(solution)/shard_map/all_to_all | solution.py:26
  175.8 8.5 %all-to-all-done.5 = bf16[4,80,1280]{2,1,0:T(8,128)(2,1)S(1)} async-done(((bf16[4,80,1280]{2,1,0:T(8,128)(2,1)}), bf16[4,80,1280]{2,1,0:T(8,128)(2,1)S(1)}, u32[]{:S(2)}, u32[]{:S(2)}) %all-to-all-start.5) | async-done | bytes 819232 | tf_op jit(solution)/shard_map/all_to_all | solution.py:26
  188.7 4.7 %copy.97 = bf16[640,8,160]{2,1,0:T(8,128)(2,1)} copy(bf16[640,8,160]{2,0,1:T(8,128)(2,1)} %bitcast.58) | data formatting | bytes 3276800 | tf_op jit(solution)/shard_map/transpose | solution.py:381
  193.4 5.2 %reshape_reshape.3 = bf16[5,8,16,1280]{3,2,1,0:T(8,128)(2,1)} reshape(bf16[640,8,160]{2,1,0:T(8,128)(2,1)} %copy.97) | data formatting | bytes 3276800 | tf_op jit(solution)/shard_map/reshape;reshape | solution.py:383
  208.6 4.8 %all-to-all-start.6 = ((bf16[8,88,160]{1,2,0:T(8,128)(2,1)}), bf16[8,88,160]{1,2,0:T(8,128)(2,1)S(1)}, u32[]{:S(2)}, u32[]{:S(2)}) async-start(bf16[8,88,160]{1,2,0:T(8,128)(2,1)} %copy.98), calls=%async_computation.6 | async-start | bytes 655360 | tf_op jit(solution)/shard_map/all_to_all | solution.py:26
  213.4 4.7 %weight_terms.1 = bf16[4,8,40,640]{3,2,1,0:T(8,128)(2,1)} custom-call(bf16[640,1280]{1,0:T(8,128)(2,1)} %get-tuple-element.23.normed_ref, bf16[640,1280]{1,0:T(8,128)(2,1)} %get-tuple-element.24.upstream_ref, bf16[640,480]{1,0:T(8,128)(2,1)} %get-tuple-element.25.packed_grad_ref, bf16[640,160]{1,0:T(8,128)(2,1)} %get-tuple-element.26.mixed_ref), custom_call_target="tpu_custom_call" | custom-call | tf_op jit(solution)/shard_map/weight_terms/pallas_call | solution.py:261
  220.2 4.7 %all-to-all-start.9 = ((bf16[4,320,640]{2,1,0:T(8,128)(2,1)}), bf16[4,320,640]{2,1,0:T(8,128)(2,1)}, u32[]{:S(2)}, u32[]{:S(2)}) async-start(bf16[4,320,640]{2,1,0:T(8,128)(2,1)} %bitcast.61), calls=%async_computation.9 | async-start | bytes 3276800 | tf_op jit(solution)/shard_map/all_to_all | solution.py:26
  225.9 20.2 %all-to-all-done.9 = bf16[4,320,640]{2,1,0:T(8,128)(2,1)} async-done(((bf16[4,320,640]{2,1,0:T(8,128)(2,1)}), bf16[4,320,640]{2,1,0:T(8,128)(2,1)}, u32[]{:S(2)}, u32[]{:S(2)}) %all-to-all-start.9) | async-done | bytes 1638432 | tf_op jit(solution)/shard_map/all_to_all | solution.py:26
  253.0 7.1 %all-to-all-done.11 = bf16[32,1,40]{2,1,0:T(2,128)(2,1)S(1)} async-done(((bf16[32,1,40]{2,1,0:T(2,128)(2,1)}), bf16[32,1,40]{2,1,0:T(2,128)(2,1)S(1)}, u32[]{:S(2)}, u32[]{:S(2)}) %all-to-all-start.11) | async-done | bytes 2592 | tf_op jit(solution)/shard_map/all_to_all | solution.py:26
  268.8 7.2 %all-to-all-done.10 = bf16[8,40,640]{2,1,0:T(8,128)(2,1)S(1)} async-done(((bf16[8,40,640]{2,1,0:T(8,128)(2,1)}), bf16[8,40,640]{2,1,0:T(8,128)(2,1)S(1)}, u32[]{:S(2)}, u32[]{:S(2)}) %all-to-all-start.10) | async-done | bytes 409632 | tf_op jit(solution)/shard_map/all_to_all | solution.py:26
  (86 shorter events, 92.6 us)
Async XLA Ops:
  0.6 2.7 copy-start
  6.4 2.5 collective-permute-start
  12.0 5.8 %copy-start.8 = (s32[32,5]{0,1:T(8,128)S(1)}, s32[32,5]{0,1:T(8,128)}, u32[]{:S(2)}) copy-start(s32[32,5]{0,1:T(8,128)} %param.12) | copy-start | bytes 1924
  12.0 31.0 %copy-start.10 = (s32[32,5]{0,1:T(8,128)S(1)}, s32[32,5]{0,1:T(8,128)}, u32[]{:S(2)}) copy-start(s32[32,5]{0,1:T(8,128)} %param.13) | copy-start | bytes 1924
  12.0 17.5 %all-to-all-start = ((bf16[4,80,1280]{2,1,0:T(8,128)(2,1)}), bf16[4,80,1280]{2,1,0:T(8,128)(2,1)S(1)}, u32[]{:S(2)}, u32[]{:S(2)}) async-start(bf16[4,80,1280]{2,1,0:T(8,128)(2,1)} %bitcast.80), calls=%async_computation | async-start | bytes 1638400 | tf_op jit(solution)/shard_map/all_to_all | solution.py:26
  32.4 30.5 %copy-start.7 = (bf16[640,160]{0,1:T(8,128)(2,1)S(1)}, bf16[640,160]{0,1:T(8,128)(2,1)}, u32[]{:S(2)}) copy-start(bf16[640,160]{0,1:T(8,128)(2,1)} %param.11) | copy-start | bytes 614404
  32.4 23.9 %all-to-all-start.1 = ((bf16[32,5,8,128]{3,2,1,0:T(8,128)(2,1)}), bf16[32,5,8,128]{3,2,1,0:T(8,128)(2,1)S(1)}, u32[]{:S(2)}, u32[]{:S(2)}) async-start(bf16[32,5,8,128]{3,2,1,0:T(8,128)(2,1)} %spread.1), calls=%async_computation.1 | async-start | bytes 655360 | tf_op jit(solution)/shard_map/all_to_all | solution.py:26
  59.0 17.2 %all-to-all-start.2 = ((bf16[32,5,8,128]{3,2,1,0:T(8,128)(2,1)}), bf16[32,5,8,128]{3,2,1,0:T(8,128)(2,1)S(1)}, u32[]{:S(2)}, u32[]{:S(2)}) async-start(bf16[32,5,8,128]{3,2,1,0:T(8,128)(2,1)} %bitcast.76), calls=%async_computation.2 | async-start | bytes 655360 | tf_op jit(solution)/shard_map/all_to_all | solution.py:26
  77.3 19.1 %copy-start.11 = (s32[5]{0:T(128)S(1)}, s32[5]{0:T(128)}, u32[]{:S(2)}) copy-start(s32[5]{0:T(128)} %dynamic-slice_reduce_fusion.counts_ref) | copy-start | bytes 64
  77.3 13.3 %all-to-all-start.4 = ((bf16[4,800,128]{2,1,0:T(8,128)(2,1)}), bf16[4,800,128]{2,1,0:T(8,128)(2,1)S(1)}, u32[]{:S(2)}, u32[]{:S(2)}) async-start(bf16[4,800,128]{2,1,0:T(8,128)(2,1)} %broadcast_in_dim.45), calls=%async_computation.4 | async-start | bytes 1638400 | tf_op jit(solution)/shard_map/all_to_all | solution.py:26
  91.4 13.1 %all-to-all-start.3 = ((bf16[4,80,1280]{2,1,0:T(8,128)(2,1)}), bf16[4,80,1280]{2,1,0:T(8,128)(2,1)S(1)}, u32[]{:S(2)}, u32[]{:S(2)}) async-start(bf16[4,80,1280]{2,1,0:T(8,128)(2,1)} %bitcast.81), calls=%async_computation.3 | async-start | bytes 1638400 | tf_op jit(solution)/shard_map/all_to_all | solution.py:26
  96.4 29.2 %collective-permute-start.2 = (bf16[4,800,128]{2,1,0:T(8,128)(2,1)}, bf16[4,800,128]{2,1,0:T(8,128)(2,1)}, u32[]{:S(2)}, u32[]{:S(2)}) collective-permute-start(bf16[4,800,128]{2,1,0:T(8,128)(2,1)} %copy-done.2), channel_id=1, source_target_pairs={{0,1},{1,0},{2,3},{3,2},{4,5},{5,4},{6,7},{7,6},{8,9},{9,8},{10,11... | collective-permute-start | bytes 2457608 | tf_op jit(solution)/shard_map/ppermute | solution.py:376
  104.6 4.4 %copy-start.1 = (bf16[4,80,1280]{2,1,0:T(8,128)(2,1)}, bf16[4,80,1280]{2,1,0:T(8,128)(2,1)S(1)}, u32[]{:S(2)}) copy-start(bf16[4,80,1280]{2,1,0:T(8,128)(2,1)S(1)} %all-to-all-done.3) | copy-start | bytes 2457604
  104.6 45.8 %collective-permute-start.1 = (bf16[4,5,16,1280]{3,2,1,0:T(8,128)(2,1)S(1)}, bf16[4,5,16,1280]{3,2,1,0:T(8,128)(2,1)}, u32[]{:S(2)}, u32[]{:S(2)}) collective-permute-start(bf16[4,5,16,1280]{3,2,1,0:T(8,128)(2,1)S(1)} %bitcast.63), channel_id=1, source_target_pairs={{0,1},{1,0},{2,3},{3,2},{4,5},{5,4},{6,7},{7,6},{8,9},{9,8},{10,11... | collective-permute-start | bytes 2457608 | tf_op jit(solution)/shard_map/ppermute | solution.py:362
  110.8 4.9 %copy-start.9 = (f32[1280]{0:T(1024)S(1)}, f32[1280]{0:T(1024)}, u32[]{:S(2)}) copy-start(f32[1280]{0:T(1024)} %param.14) | copy-start | bytes 15364
  110.8 56.7 %all-to-all-start.7 = ((bf16[4,320,1024]{2,1,0:T(8,128)(2,1)}), bf16[4,320,1024]{2,1,0:T(8,128)(2,1)}, u32[]{:S(2)}, u32[]{:S(2)}) async-start(bf16[4,320,1024]{2,1,0:T(8,128)(2,1)} %bitcast.59), calls=%async_computation.7 | async-start | bytes 5242880 | tf_op jit(solution)/shard_map/all_to_all | solution.py:26
  162.7 2.6 collective-permute-start.3
  167.6 16.8 %all-to-all-start.5 = ((bf16[4,80,1280]{2,1,0:T(8,128)(2,1)}), bf16[4,80,1280]{2,1,0:T(8,128)(2,1)S(1)}, u32[]{:S(2)}, u32[]{:S(2)}) async-start(bf16[4,80,1280]{2,1,0:T(8,128)(2,1)} %bitcast.22), calls=%async_computation.5 | async-start | bytes 1638400 | tf_op jit(solution)/shard_map/all_to_all | solution.py:26
  184.3 9.0 %copy-start.4 = (bf16[4,80,1280]{2,1,0:T(8,128)(2,1)}, bf16[4,80,1280]{2,1,0:T(8,128)(2,1)S(1)}, u32[]{:S(2)}) copy-start(bf16[4,80,1280]{2,1,0:T(8,128)(2,1)S(1)} %all-to-all-done.5) | copy-start | bytes 2457604
  184.3 24.3 %all-to-all-start.8 = ((bf16[8,40,1024]{2,1,0:T(8,128)(2,1)}), bf16[8,40,1024]{2,1,0:T(8,128)(2,1)}, u32[]{:S(2)}, u32[]{:S(2)}) async-start(bf16[8,40,1024]{2,1,0:T(8,128)(2,1)} %bitcast.70), calls=%async_computation.8 | async-start | bytes 1310720 | tf_op jit(solution)/shard_map/all_to_all | solution.py:26
  208.6 11.6 %all-to-all-start.6 = ((bf16[8,88,160]{1,2,0:T(8,128)(2,1)}), bf16[8,88,160]{1,2,0:T(8,128)(2,1)S(1)}, u32[]{:S(2)}, u32[]{:S(2)}) async-start(bf16[8,88,160]{1,2,0:T(8,128)(2,1)} %copy.98), calls=%async_computation.6 | async-start | bytes 655360 | tf_op jit(solution)/shard_map/all_to_all | solution.py:26
  220.2 25.9 %all-to-all-start.9 = ((bf16[4,320,640]{2,1,0:T(8,128)(2,1)}), bf16[4,320,640]{2,1,0:T(8,128)(2,1)}, u32[]{:S(2)}, u32[]{:S(2)}) async-start(bf16[4,320,640]{2,1,0:T(8,128)(2,1)} %bitcast.61), calls=%async_computation.9 | async-start | bytes 3276800 | tf_op jit(solution)/shard_map/all_to_all | solution.py:26
  246.1 14.0 %all-to-all-start.11 = ((bf16[32,1,40]{2,1,0:T(2,128)(2,1)}), bf16[32,1,40]{2,1,0:T(2,128)(2,1)S(1)}, u32[]{:S(2)}, u32[]{:S(2)}) async-start(bf16[32,1,40]{2,1,0:T(2,128)(2,1)} %reshape.187), calls=%async_computation.11 | async-start | bytes 32768 | tf_op jit(solution)/shard_map/all_to_all | solution.py:26
  260.1 15.8 %all-to-all-start.10 = ((bf16[8,40,640]{2,1,0:T(8,128)(2,1)}), bf16[8,40,640]{2,1,0:T(8,128)(2,1)S(1)}, u32[]{:S(2)}, u32[]{:S(2)}) async-start(bf16[8,40,640]{2,1,0:T(8,128)(2,1)} %bitcast.71), calls=%async_computation.10 | async-start | bytes 819200 | tf_op jit(solution)/shard_map/all_to_all | solution.py:26
  (4 other events, 3.6 us)
